TPU v7x, 32 devices: a whole 2x2x4 slice. The times are simulated.
32 devices in a mesh: rep: 4 (over z), seq: 8 (over y, x, core).
Axes of the slice: x: 2, y: 2, z: 4, core: 2. Of those that a mesh axis runs over, the one named last changes fastest.
Arguments:
- frames_in: bfloat16 [4, 8, 4, 128, 1152], P('rep', 'seq'), may hold values from -6 to 6
- conditioning: float32 [4, 1152], P('rep'), may hold values from -6 to 6
- mod_first: bfloat16 [1152, 6912], P('seq'), may hold values from -0.1875 to 0.1875
- qkv_first: bfloat16 [1152, 3456], P('seq'), may hold values from -0.1875 to 0.1875
- out_first: bfloat16 [1152, 1152], P('seq'), may hold values from -0.75 to 0.75
- up_first: bfloat16 [1152, 4608], P('seq'), may hold values from -0.1875 to 0.1875
- down_first: bfloat16 [4608, 1152], P('seq'), may hold values from -0.09375 to 0.09375
- mod_second: bfloat16 [1152, 6912], P('seq'), may hold values from -0.1875 to 0.1875
- qkv_second: bfloat16 [1152, 3456], P('seq'), may hold values from -0.1875 to 0.1875
- out_second: bfloat16 [1152, 1152], P('seq'), may hold values from -0.375 to 0.375
- up_second: bfloat16 [1152, 4608], P('seq'), may hold values from -0.1875 to 0.1875
- down_second: bfloat16 [4608, 1152], P('seq'), may hold values from -0.09375 to 0.09375
- cotangent: float32 [4, 8, 4, 128, 1152], P('rep', 'seq'), may hold values from -6 to 6
Outputs:
- block_out: float32 [4, 8, 4, 128, 1152], P('rep', 'seq')
- input_grad: float32 [4, 8, 4, 128, 1152], P('rep', 'seq')
- conditioning_grad: float32 [4, 1152], P('rep', 'seq')
- mod_first_grad: float32 [1152, 6912], P('seq')
- qkv_first_grad: float32 [1152, 3456], P('seq')
- out_first_grad: float32 [1152, 1152], P('seq')
- up_first_grad: float32 [1152, 4608], P('seq')
- first_down_gradient: float32 [4608, 1152], P('seq')
- mod_second_grad: float32 [1152, 6912], P('seq')
- qkv_second_grad: float32 [1152, 3456], P('seq')
- out_second_grad: float32 [1152, 1152], P('seq')
- up_second_grad: float32 [1152, 4608], P('seq')
- down_second_grad: float32 [4608, 1152], P('seq')
All inputs are finite; a program needn't handle non-finite values.
Results may differ from a plain program's by a relative error of at most 0.02175.
Values may be sent and summed in bfloat16 or wider, within the bound.
A program may use at most 384 MiB of HBM per device.

v0:
```python
import jax
import jax.numpy as jnp
from jax import lax
from jax.sharding import PartitionSpec as P

HEADS = 16
HEAD_WIDTH = 72
norm_epsilon = 1e-06


def from_partner(block, axis, apart):
    count = lax.axis_size(axis)
    route = []
    for low in range(count):
        high = low | 1 << apart
        if high != low and high < count:
            route += [(low, high), (high, low)]
    return lax.ppermute(block, axis, route)


def shortened(x):
    return jax.tree.map(lambda a: a.astype(jnp.bfloat16) if a.dtype == jnp.float32 else a, x)


def layer_mod(stream, shift_part, scale_part):
    row_mean = jnp.mean(stream, axis=-1, keepdims=True)
    centred = stream - row_mean
    row_var = jnp.mean(centred * centred, axis=-1, keepdims=True)
    return centred * lax.rsqrt(row_var + norm_epsilon) * (1.0 + scale_part) + shift_part


def gelu_tanh(pre_value):
    return jax.nn.gelu(pre_value, approximate=True)


def project(left_operand, right_operand):
    return jnp.einsum(
        "csld,de->csle", left_operand, right_operand, preferred_element_type=jnp.float32
    )


def project_back(incoming, right_operand):
    return jnp.einsum("csle,de->csld", incoming, right_operand, preferred_element_type=jnp.float32)


def mod_parts(modulation):
    return [segment[:, None, None, :] for segment in jnp.split(modulation, 6, axis=-1)]


def modulations(conditioning, mod_one, mod_two):
    row_count = mod_one.shape[0]
    row_start = lax.axis_index("seq") * row_count
    silu_local = lax.dynamic_slice_in_dim(
        jax.nn.silu(conditioning), row_start, row_count, 1
    ).astype(jnp.bfloat16)
    part_one = jnp.dot(silu_local, mod_one, preferred_element_type=jnp.float32)
    part_two = jnp.dot(silu_local, mod_two, preferred_element_type=jnp.float32)
    summed = lax.psum((part_one, part_two), "seq")
    return (summed[0], summed[1], silu_local, row_start)


def gather_layer(qkv_w, out_w, up_w, down_w):
    return (
        lax.all_gather(qkv_w, "seq", axis=0, tiled=True),
        lax.all_gather(out_w, "seq", axis=0, tiled=True),
        lax.all_gather(up_w, "seq", axis=0, tiled=True),
        lax.all_gather(down_w, "seq", axis=0, tiled=True),
    )


def gather_layer_again(qkv_w, out_w, up_w, down_w):
    return (
        lax.all_gather(qkv_w, "seq", axis=0, tiled=True),
        lax.all_gather(out_w, "seq", axis=0, tiled=True),
        lax.all_gather(up_w, "seq", axis=0, tiled=True),
        lax.all_gather(down_w, "seq", axis=0, tiled=True),
    )


def partner_values(stacked):
    return from_partner(stacked, "seq", 0)


def partner_grads(stacked):
    return from_partner(stacked.astype(jnp.bfloat16), "seq", 0).astype(stacked.dtype)


def to_places(stream):
    clip_count, frame_dev, half_places, features = stream.shape
    devices = lax.axis_size("seq")
    place_part = half_places // devices
    exchanged = lax.all_to_all(
        stream.reshape(1, clip_count, frame_dev, devices, place_part, features).astype(
            jnp.bfloat16
        ),
        "seq",
        split_axis=3,
        concat_axis=0,
        tiled=True,
    ).astype(jnp.float32)
    exchanged = exchanged.reshape(devices // 2, 2, clip_count, frame_dev, place_part, features)
    exchanged = jnp.transpose(exchanged, (2, 1, 4, 0, 3, 5))
    return exchanged.reshape(clip_count, 2 * place_part, devices // 2 * frame_dev, features)


def to_frames(stream, frame_dev):
    clip_count, place_count, frame_total, features = stream.shape
    devices = lax.axis_size("seq")
    place_part = place_count // 2
    arranged = stream.reshape(clip_count, 2, place_part, devices // 2, frame_dev, features)
    arranged = jnp.transpose(arranged, (3, 1, 0, 4, 2, 5)).reshape(
        devices, clip_count, frame_dev, 1, place_part, features
    )
    exchanged = lax.all_to_all(
        shortened(arranged), "seq", split_axis=0, concat_axis=3, tiled=True
    ).astype(arranged.dtype)
    return exchanged.reshape(clip_count, frame_dev, devices * place_part, features)


def forward_layer(stream, modulation, weights, spatial):
    qkv_w, out_w, up_w, down_w = weights
    shift_attn, scale_attn, gate_attn, shift_mlp, scale_mlp, gate_mlp = mod_parts(modulation)
    clip_count, seq_count, seq_len, features = stream.shape
    normed = layer_mod(stream, shift_attn, scale_attn).astype(jnp.bfloat16)
    projected = project(normed, qkv_w).astype(jnp.bfloat16)
    queries, keys_all, values_all = jnp.split(projected, 3, axis=-1)
    if spatial:
        remote = partner_values(jnp.stack([keys_all, values_all]))
        keys_all = jnp.concatenate([keys_all, remote[0]], axis=2)
        values_all = jnp.concatenate([values_all, remote[1]], axis=2)
    key_len = keys_all.shape[2]
    queries = queries.reshape(clip_count, seq_count, seq_len, HEADS, HEAD_WIDTH)
    keys_all = keys_all.reshape(clip_count, seq_count, key_len, HEADS, HEAD_WIDTH)
    values_all = values_all.reshape(clip_count, seq_count, key_len, HEADS, HEAD_WIDTH)
    scores = jnp.einsum(
        "cslhe,csmhe->cshlm", queries, keys_all, preferred_element_type=jnp.float32
    ) * HEAD_WIDTH ** (-0.5)
    peak_score = jnp.max(scores, axis=-1, keepdims=True)
    scaled_exp = jnp.exp(scores - peak_score)
    attention = scaled_exp / jnp.sum(scaled_exp, axis=-1, keepdims=True)
    attention_low = attention.astype(jnp.bfloat16)
    attended = jnp.einsum(
        "cshlm,csmhe->cslhe", attention_low, values_all, preferred_element_type=jnp.float32
    )
    attended = attended.astype(jnp.bfloat16).reshape(clip_count, seq_count, seq_len, features)
    branch = project(attended, out_w)
    middle = stream + gate_attn * branch
    normed_mid = layer_mod(middle, shift_mlp, scale_mlp).astype(jnp.bfloat16)
    hidden_pre = project(normed_mid, up_w)
    hidden = gelu_tanh(hidden_pre).astype(jnp.bfloat16)
    mlp_out = project(hidden, down_w)
    result = middle + gate_mlp * mlp_out
    kept_state = (
        normed,
        queries,
        keys_all,
        values_all,
        attention,
        attention_low,
        attended,
        branch,
        middle,
        normed_mid,
        hidden_pre,
        hidden,
        mlp_out,
    )
    return (result, kept_state)


def backward_layer(result_grad, stream, modulation, weights, kept_state, spatial):
    qkv_w, out_w, up_w, down_w = weights
    (
        normed,
        queries,
        keys_all,
        values_all,
        attention,
        attention_low,
        attended,
        branch,
        middle,
        normed_mid,
        hidden_pre,
        hidden,
        mlp_out,
    ) = kept_state
    shift_attn, scale_attn, gate_attn, shift_mlp, scale_mlp, gate_mlp = mod_parts(modulation)
    clip_count, seq_count, seq_len, features = stream.shape
    gate_mlp_grad = jnp.sum(result_grad * mlp_out, axis=(1, 2))
    mlp_grad = (gate_mlp * result_grad).astype(jnp.bfloat16)
    hidden_grad = project_back(mlp_grad, down_w)
    pre_grad = jax.vjp(gelu_tanh, hidden_pre)[1](hidden_grad)[0].astype(jnp.bfloat16)
    normed_mid_grad = project_back(pre_grad, up_w)
    middle_ln_grad, shift_mlp_grad, scale_mlp_grad = jax.vjp(
        layer_mod, middle, shift_mlp, scale_mlp
    )[1](normed_mid_grad)
    middle_grad = result_grad + middle_ln_grad
    gate_attn_grad = jnp.sum(middle_grad * branch, axis=(1, 2))
    branch_grad = (gate_attn * middle_grad).astype(jnp.bfloat16)
    attended_grad = project_back(branch_grad, out_w).astype(jnp.bfloat16)
    attended_grad = attended_grad.reshape(clip_count, seq_count, seq_len, HEADS, HEAD_WIDTH)
    attention_grad = jnp.einsum(
        "cslhe,csmhe->cshlm", attended_grad, values_all, preferred_element_type=jnp.float32
    )
    scores_grad = attention * (
        attention_grad - jnp.sum(attention_grad * attention, axis=-1, keepdims=True)
    )
    scores_grad = scores_grad.astype(jnp.bfloat16)
    inv_root = HEAD_WIDTH ** (-0.5)
    queries_grad = (
        jnp.einsum("cshlm,csmhe->cslhe", scores_grad, keys_all, preferred_element_type=jnp.float32)
        * inv_root
    )
    keys_grad = (
        jnp.einsum("cshlm,cslhe->csmhe", scores_grad, queries, preferred_element_type=jnp.float32)
        * inv_root
    )
    values_grad = jnp.einsum(
        "cshlm,cslhe->csmhe", attention_low, attended_grad, preferred_element_type=jnp.float32
    )
    if spatial:
        returned = partner_grads(
            jnp.stack([keys_grad[:, :, seq_len:], values_grad[:, :, seq_len:]])
        )
        keys_grad = keys_grad[:, :, :seq_len] + returned[0]
        values_grad = values_grad[:, :, :seq_len] + returned[1]
    qkv_grad = jnp.concatenate(
        [
            component.reshape(clip_count, seq_count, seq_len, features)
            for component in (queries_grad, keys_grad, values_grad)
        ],
        axis=-1,
    )
    qkv_grad = qkv_grad.astype(jnp.bfloat16)
    normed_grad = project_back(qkv_grad, qkv_w)
    stream_ln_grad, attention_shift_gradient, scale_attn_grad = jax.vjp(
        layer_mod, stream, shift_attn, scale_attn
    )[1](normed_grad)
    stream_grad = middle_grad + stream_ln_grad
    mod_grad = jnp.concatenate(
        [
            attention_shift_gradient.reshape(clip_count, features),
            scale_attn_grad.reshape(clip_count, features),
            gate_attn_grad,
            shift_mlp_grad.reshape(clip_count, features),
            scale_mlp_grad.reshape(clip_count, features),
            gate_mlp_grad,
        ],
        axis=-1,
    )
    grad_pairs = (
        (normed, qkv_grad),
        (attended, branch_grad),
        (normed_mid, pre_grad),
        (hidden, mlp_grad),
    )
    return (stream_grad, mod_grad, grad_pairs)


def spread_rows_out(left_operand, right_operand):
    left_flat = left_operand.reshape(-1, left_operand.shape[-1])
    right_flat = right_operand.reshape(-1, right_operand.shape[-1])
    return lax.psum_scatter(
        jnp.einsum("nd,ne->de", left_flat, right_flat, preferred_element_type=jnp.float32).astype(
            jnp.bfloat16
        ),
        "seq",
        scatter_dimension=0,
        tiled=True,
    ).astype(jnp.float32)


def layer_grads(grad_pairs):
    return tuple(
        (spread_rows_out(grad_pairs[index][0], grad_pairs[index][1]) for index in range(4))
    )


def per_device(
    frames_in,
    conditioning,
    mod_first,
    qkv_first,
    out_first,
    up_first,
    down_first,
    mod_second,
    qkv_second,
    out_second,
    up_second,
    down_second,
    cotangent,
):
    clip_count = frames_in.shape[0]
    frame_dev = frames_in.shape[2]
    half_places = frames_in.shape[3]
    features = frames_in.shape[4]
    start_stream = frames_in.reshape(clip_count, frame_dev, half_places, features).astype(
        jnp.float32
    )
    mod_one, mod_two, silu_local, row_start = modulations(conditioning, mod_first, mod_second)
    weights_one = gather_layer(qkv_first, out_first, up_first, down_first)
    spatial_out, unused_one = forward_layer(start_stream, mod_one, weights_one, True)
    weights_two = gather_layer(qkv_second, out_second, up_second, down_second)
    temporal_out, unused_two = forward_layer(to_places(spatial_out), mod_two, weights_two, False)
    block_out = to_frames(temporal_out, frame_dev)
    mod_one, mod_two, silu_local, row_start = modulations(conditioning, mod_first, mod_second)
    again_one = gather_layer_again(qkv_first, out_first, up_first, down_first)
    spatial_again, state_one = forward_layer(start_stream, mod_one, again_one, True)
    again_two = gather_layer_again(qkv_second, out_second, up_second, down_second)
    placed_again = to_places(spatial_again)
    unused_three, state_two = forward_layer(placed_again, mod_two, again_two, False)
    cotangent_sites = to_places(cotangent.reshape(clip_count, frame_dev, half_places, features))
    placed_grad, mod_grad_two, pairs_two = backward_layer(
        cotangent_sites, placed_again, mod_two, again_two, state_two, False
    )
    row_attn = qkv_first.shape[0]
    grads_two = layer_grads(pairs_two)
    spatial_grad = to_frames(placed_grad, frame_dev)
    stream_grad, mod_grad_one, pairs_one = backward_layer(
        spatial_grad, start_stream, mod_one, again_one, state_one, True
    )
    grads_one = layer_grads(pairs_one)
    mod_totals = (
        lax.psum(mod_grad_one.astype(jnp.bfloat16), "seq").astype(jnp.float32),
        lax.psum(mod_grad_two.astype(jnp.bfloat16), "seq").astype(jnp.float32),
    )
    low_one = mod_totals[0].astype(jnp.bfloat16)
    low_two = mod_totals[1].astype(jnp.bfloat16)
    mod_weight_one = jnp.einsum(
        "cd,ce->de", silu_local, low_one, preferred_element_type=jnp.float32
    )
    mod_weight_two = jnp.einsum(
        "cd,ce->de", silu_local, low_two, preferred_element_type=jnp.float32
    )
    silu_grad = jnp.einsum("ce,de->cd", low_one, mod_first, preferred_element_type=jnp.float32)
    silu_grad = silu_grad + jnp.einsum(
        "ce,de->cd", low_two, mod_second, preferred_element_type=jnp.float32
    )
    condition_local = lax.dynamic_slice_in_dim(conditioning, row_start, row_attn, 1)
    condition_grad = jax.vjp(jax.nn.silu, condition_local)[1](silu_grad)[0]
    summed = (
        lax.psum(mod_weight_one.astype(jnp.bfloat16), "rep").astype(jnp.float32),
        lax.psum(grads_one[0].astype(jnp.bfloat16), "rep").astype(jnp.float32),
        lax.psum(grads_one[1].astype(jnp.bfloat16), "rep").astype(jnp.float32),
        lax.psum(grads_one[2].astype(jnp.bfloat16), "rep").astype(jnp.float32),
        lax.psum(grads_one[3].astype(jnp.bfloat16), "rep").astype(jnp.float32),
        lax.psum(mod_weight_two.astype(jnp.bfloat16), "rep").astype(jnp.float32),
        lax.psum(grads_two[0].astype(jnp.bfloat16), "rep").astype(jnp.float32),
        lax.psum(grads_two[1].astype(jnp.bfloat16), "rep").astype(jnp.float32),
        lax.psum(grads_two[2].astype(jnp.bfloat16), "rep").astype(jnp.float32),
        lax.psum(grads_two[3].astype(jnp.bfloat16), "rep").astype(jnp.float32),
    )
    out_shape = (clip_count, 1, frame_dev, half_places, features)
    return (
        block_out.reshape(out_shape),
        stream_grad.reshape(out_shape),
        condition_grad,
        summed[0],
        summed[1],
        summed[2],
        summed[3],
        summed[4],
        summed[5],
        summed[6],
        summed[7],
        summed[8],
        summed[9],
    )


def solution(mesh):
    return jax.shard_map(
        per_device,
        mesh=mesh,
        in_specs=(
            P("rep", "seq", None, None, None),
            P("rep", None),
            P("seq", None),
            P("seq", None),
            P("seq", None),
            P("seq", None),
            P("seq", None),
            P("seq", None),
            P("seq", None),
            P("seq", None),
            P("seq", None),
            P("seq", None),
            P("rep", "seq", None, None, None),
        ),
        out_specs=(
            P("rep", "seq", None, None, None),
            P("rep", "seq", None, None, None),
            P("rep", "seq"),
            P("seq", None),
            P("seq", None),
            P("seq", None),
            P("seq", None),
            P("seq", None),
            P("seq", None),
            P("seq", None),
            P("seq", None),
            P("seq", None),
            P("seq", None),
        ),
        check_vma=False,
    )
```

profile of v0, /device:TPU:0, one launch (start us, length us, event | category | flops | bytes accessed | tf_op | source)
XLA Modules:
  0.0 1629.8 jit_solution(10004412810075176240)
XLA Ops:
  17.6 26.8 %all-reduce = (f32[1,6912]{1,0:T(1,128)S(1)}, f32[1,6912]{1,0:T(1,128)S(1)}) all-reduce(f32[1,6912]{1,0:T(1,128)S(1)} %fusion.149, f32[1,6912]{1,0:T(1,128)S(1)} %fusion.147), channel_id=1, replica_groups=mesh['rep'=4,'seq'=8] {'seq'}, use_global_device_ids=true, to_apply=%region_0.1 | all-reduce | flops 13824 | bytes 110592 | tf_op jit(solution)/shard_map/psum | solution.py:58
  44.6 21.0 %all-gather.9.cloned.1.call-done = bf16[1152,3456]{1,0:T(8,128)(2,1)} async-done(((bf16[144,3456]{1,0:T(8,128)(2,1)}), bf16[1152,3456]{1,0:T(8,128)(2,1)}) %all-gather.9.cloned.1.call-update) | async-done | bytes 7962640 | tf_op jit(solution)/shard_map/all_gather | solution.py:64
  109.1 22.1 %fusion.119 = bf16[4,16,72,128]{3,2,1,0:T(8,128)(2,1)} fusion(bf16[1,4,128,16,72]{2,4,3,1,0:T(8,128)(2,1)} %bitcast.356, bf16[1,4,128,16,72]{2,4,3,1,0:T(8,128)(2,1)} %bitcast.354, f32[4,16,128]{2,1,0:T(8,128)S(1)} %get-tuple-element.81, f32[4,16,128,256]{3,2,1,0:T(8,128)} %copy-done.5), kind=kOutput, calls=%fused_computation.180 | convolution fusion | flops 317792512 | bytes 11960320 | tf_op jit(solution)/shard_map/cshlm,csmhe->cslhe/dot_general | solution.py:142
  138.6 36.5 %all-gather.13.cloned.1.call-done = bf16[1152,4608]{1,0:T(8,128)(2,1)} async-done(((bf16[144,4608]{1,0:T(8,128)(2,1)}), bf16[1152,4608]{1,0:T(8,128)(2,1)}) %all-gather.13.cloned.1.call-update) | async-done | bytes 10616848 | tf_op jit(solution)/shard_map/all_gather | solution.py:66
  175.1 23.9 %fusion.22 = f32[4,128,4608]{2,1,0:T(8,128)} fusion(bf16[1152,4608]{1,0:T(8,128)(2,1)} %all-gather.13.cloned.1.call-done, f32[4,128,1152]{2,1,0:T(8,128)} %copy-done.3, f32[1152]{0:T(1024)S(1)} %get-tuple-element.32, f32[1152]{0:T(1024)S(1)} %get-tuple-element.33, f32[4,128]{1,0:T(4,128)S(1)} %fusion.144, f32[4,128]{1,0:T(4,128)S(1)} %broadcast_multiply_fusion.2), kind=kOutput, calls=%fused_computation.32 | convolution fusion | flops 5438767104 | bytes 22426624 | tf_op jit(solution)/shard_map/csld,de->csle/dot_general | solution.py:37
  199.1 41.6 %all-gather.15.cloned.1.call-done = bf16[4608,1152]{1,0:T(8,128)(2,1)} async-done(((bf16[576,1152]{1,0:T(8,128)(2,1)}), bf16[4608,1152]{1,0:T(8,128)(2,1)}) %all-gather.15.cloned.1.call-update) | async-done | bytes 10616848 | tf_op jit(solution)/shard_map/all_gather | solution.py:67
  240.7 13.8 add_convert_fusion.4
  330.9 16.3 %fusion.179 = (f32[32,16,16]{2,1,0:T(8,128)S(1)}, f32[32,16,16,16]{2,3,1,0:T(8,128)S(1)}) fusion(f32[32,16,16,16]{2,3,1,0:T(8,128)S(1)} %fusion.109), kind=kOutput, calls=%fused_computation.279 | output fusion | flops 524303 | bytes 1081344 | tf_op jit(solution)/shard_map/sub | solution.py:139
  363.9 34.0 %all-gather.21.cloned.1.call-done = bf16[1152,4608]{1,0:T(8,128)(2,1)} async-done(((bf16[144,4608]{1,0:T(8,128)(2,1)}), bf16[1152,4608]{1,0:T(8,128)(2,1)}) %all-gather.21.cloned.1.call-update) | async-done | bytes 10616848 | tf_op jit(solution)/shard_map/all_gather | solution.py:66
  397.9 13.2 fusion.14
  411.1 52.6 %all-gather.23.cloned.1.call-done = bf16[4608,1152]{1,0:T(8,128)(2,1)} async-done(((bf16[576,1152]{1,0:T(8,128)(2,1)}), bf16[4608,1152]{1,0:T(8,128)(2,1)}) %all-gather.23.cloned.1.call-update) | async-done | bytes 10616848 | tf_op jit(solution)/shard_map/all_gather | solution.py:67
  463.7 16.0 fusion.37
  479.6 13.5 multiply_reduce_fusion.13
  497.5 18.1 %multiply_reduce_fusion.4 = (bf16[1152]{0:T(1024)(128)(2,1)}, bf16[32,16,1152]{2,1,0:T(8,128)(2,1)}, bf16[1152]{0:T(1024)(128)(2,1)}, f32[32,16,1152]{2,1,0:T(8,128)S(1)}) fusion(f32[32,16,1152]{2,1,0:T(8,128)} %reshape.1279, f32[32,16,1152]{2,1,0:T(8,128)} %get-tuple-element.59, f32[1152]{0:T(1024)S(1)} %get-tuple-element.25, ...), kind=kOutput, calls=%fused_computation.133 | convolution fusion | flops 5465896960 | bytes 33052160 | tf_op jit(solution)/shard_map/csld,de->csle/dot_general | solution.py:37
  563.1 10.9 multiply_reduce_fusion.12
  606.5 17.4 %fusion.30 = bf16[4,128,4608]{2,1,0:T(8,128)(2,1)} fusion(f32[4,128,4608]{2,1,0:T(8,128)} %fusion.22, bf16[4608,1152]{1,0:T(8,128)(2,1)} %all-gather.15.cloned.1.call-done, f32[4,128,1152]{2,1,0:T(8,128)S(1)} %bitcast.337, f32[1152]{0:T(1024)S(1)} %copy-done.64), kind=kOutput, calls=%fused_computation.40 | convolution fusion | flops 5484183552 | bytes 27136512 | tf_op jit(solution)/shard_map/csle,de->csld/dot_general | solution.py:43
  624.0 11.9 multiply_reduce_fusion.11
  646.3 10.6 fusion.7
  664.3 22.2 %convolution_bitcast_fusion.6 = f32[1,4,256,16,72]{2,4,3,1,0:T(8,128)} fusion(bf16[4,128,16,72]{1,3,2,0:T(8,128)(2,1)} %bitcast.360, f32[4,16,128]{2,1,0:T(8,128)S(1)} %copy-done.54, f32[4,16,128,256]{3,2,1,0:T(8,128)} %copy-done.5), kind=kOutput, calls=%fused_computation.161 | convolution fusion | flops 312484096 | bytes 14319616 | tf_op jit(solution)/shard_map/cshlm,cslhe->csmhe/dot_general | solution.py:219
  732.1 13.0 fusion.3
  745.8 11.2 fusion.2
  758.5 12.1 fusion.5
  771.3 11.5 fusion.4
  784.2 10.9 fusion.85
  797.8 23.5 %all-reduce.1 = (bf16[6912]{0:T(1024)(128)(2,1)S(1)}, bf16[6912]{0:T(1024)(128)(2,1)S(1)}) all-reduce(bf16[6912]{0:T(1024)(128)(2,1)S(1)} %reduce.79, bf16[6912]{0:T(1024)(128)(2,1)S(1)} %reduce.80), channel_id=1, replica_groups=mesh['rep'=4,'seq'=8] {'seq'}, use_global_device_ids=true, to_apply=%region_30.31 | all-reduce | flops 13824 | bytes 55296 | tf_op jit(solution)/shard_map/psum | solution.py:326
  823.8 20.3 %reduce-scatter.9.cloned.1.call-done = bf16[144,3456]{1,0:T(8,128)(2,1)} async-done(((bf16[1152,3456]{1,0:T(8,128)(2,1)}), bf16[144,3456]{1,0:T(8,128)(2,1)}) %reduce-scatter.9.cloned.1.call-update) | async-done | bytes 995344 | tf_op jit(solution)/shard_map/reduce_scatter | solution.py:264
  844.1 85.7 %reduce-scatter.23.cloned.1.call-done = bf16[576,1152]{1,0:T(8,128)(2,1)} async-done(((bf16[4608,1152]{1,0:T(8,128)(2,1)}), bf16[576,1152]{1,0:T(8,128)(2,1)}) %reduce-scatter.23.cloned.1.call-update) | async-done | bytes 1327120 | tf_op jit(solution)/shard_map/reduce_scatter | solution.py:264
  929.8 85.6 %reduce-scatter.21.cloned.1.call-done = bf16[144,4608]{1,0:T(8,128)(2,1)} async-done(((bf16[1152,4608]{1,0:T(8,128)(2,1)}), bf16[144,4608]{1,0:T(8,128)(2,1)}) %reduce-scatter.21.cloned.1.call-update) | async-done | bytes 1327120 | tf_op jit(solution)/shard_map/reduce_scatter | solution.py:264
  1015.4 85.6 %reduce-scatter.15.cloned.1.call-done = bf16[576,1152]{1,0:T(8,128)(2,1)} async-done(((bf16[4608,1152]{1,0:T(8,128)(2,1)}), bf16[576,1152]{1,0:T(8,128)(2,1)}) %reduce-scatter.15.cloned.1.call-update) | async-done | bytes 1327120 | tf_op jit(solution)/shard_map/reduce_scatter | solution.py:264
  1101.0 85.6 %reduce-scatter.13.cloned.1.call-done = bf16[144,4608]{1,0:T(8,128)(2,1)} async-done(((bf16[1152,4608]{1,0:T(8,128)(2,1)}), bf16[144,4608]{1,0:T(8,128)(2,1)}) %reduce-scatter.13.cloned.1.call-update) | async-done | bytes 1327120 | tf_op jit(solution)/shard_map/reduce_scatter | solution.py:264
  1191.4 19.3 %all_to_all.16 = bf16[8,1,4,1,16,1152]{5,4,2,3,1,0:T(8,128)(2,1)S(1)} all-to-all(bf16[8,1,4,1,16,1152]{5,4,2,3,1,0:T(8,128)(2,1)S(1)} %bitcast.348), channel_id=1, replica_groups=mesh['rep'=4,'seq'=8] {'seq'}, dimensions={0} | all-to-all | bytes 2359296 | tf_op jit(solution)/shard_map/all_to_all | solution.py:114
  1217.3 386.7 %all-reduce.5.cloned.1.call-done = (bf16[144,6912]{1,0:T(8,128)(2,1)}, bf16[144,3456]{1,0:T(8,128)(2,1)}, bf16[144,1152]{1,0:T(8,128)(2,1)}, bf16[144,4608]{1,0:...) async-done(((bf16[144,6912]{1,0:T(8,128)(2,1)}, ...) | async-done | bytes 11943952 | tf_op jit(solution)/shard_map/psum | solution.py:344
  (435 shorter events, 340.9 us)
Async XLA Ops:
  7.2 58.4 %all-gather.9.cloned.1.call-start = ((), (), s32[]{:S(2)}) async-start(), calls=%async_computation.12 | async-start | bytes 8957952 | tf_op jit(solution)/shard_map/all_gather | solution.py:64
  7.9 123.3 %all-gather.11.cloned.1.call-start = ((), (), s32[]{:S(2)}) async-start(), calls=%async_computation.13 | async-start | bytes 2985984 | tf_op jit(solution)/shard_map/all_gather | solution.py:65
  8.7 166.4 %all-gather.13.cloned.1.call-start = ((), (), s32[]{:S(2)}) async-start(), calls=%async_computation.14 | async-start | bytes 11943936 | tf_op jit(solution)/shard_map/all_gather | solution.py:66
  9.4 231.3 %all-gather.15.cloned.1.call-start = ((), (), s32[]{:S(2)}) async-start(), calls=%async_computation.15 | async-start | bytes 11943936 | tf_op jit(solution)/shard_map/all_gather | solution.py:67
  10.0 290.4 %all-gather.17.cloned.1.call-start = ((), (), s32[]{:S(2)}) async-start(), calls=%async_computation.16 | async-start | bytes 8957952 | tf_op jit(solution)/shard_map/all_gather | solution.py:64
  10.6 344.4 %all-gather.19.cloned.1.call-start = ((), (), s32[]{:S(2)}) async-start(), calls=%async_computation.17 | async-start | bytes 2985984 | tf_op jit(solution)/shard_map/all_gather | solution.py:65
  11.2 386.8 %all-gather.21.cloned.1.call-start = ((), (), s32[]{:S(2)}) async-start(), calls=%async_computation.18 | async-start | bytes 11943936 | tf_op jit(solution)/shard_map/all_gather | solution.py:66
  11.9 451.7 %all-gather.23.cloned.1.call-start = ((), (), s32[]{:S(2)}) async-start(), calls=%async_computation.19 | async-start | bytes 11943936 | tf_op jit(solution)/shard_map/all_gather | solution.py:67
  44.6 86.6 %copy-start.49 = (f32[1152]{0:T(1024)}, f32[1152]{0:T(1024)S(1)}, u32[]{:S(2)}) copy-start(f32[1152]{0:T(1024)S(1)} %get-tuple-element.36) | copy-start | bytes 13828
  44.6 130.5 %copy-start.55 = (f32[1152]{0:T(1024)}, f32[1152]{0:T(1024)S(1)}, u32[]{:S(2)}) copy-start(f32[1152]{0:T(1024)S(1)} %get-tuple-element.33) | copy-start | bytes 13828
  44.6 130.5 %copy-start.94 = (f32[1152]{0:T(1024)}, f32[1152]{0:T(1024)S(1)}, u32[]{:S(2)}) copy-start(f32[1152]{0:T(1024)S(1)} %get-tuple-element.32) | copy-start | bytes 13828
  44.6 196.1 %copy-start.63 = (f32[1152]{0:T(1024)}, f32[1152]{0:T(1024)S(1)}, u32[]{:S(2)}) copy-start(f32[1152]{0:T(1024)S(1)} %get-tuple-element.31) | copy-start | bytes 13828
  78.1 13.9 collective-permute-start
  80.2 175.4 %all-to-all-start.2 = ((bf16[1,1,4,8,16,1152]{5,4,2,1,0,3:T(8,128)(2,1)}), bf16[1,1,4,8,16,1152]{5,4,2,1,0,3:T(8,128)(2,1)}, u32[]{:S(2)}, u32[]{:S(2)}) async-start(bf16[1,1,4,8,16,1152]{5,4,2,1,0,3:T(8,128)(2,1)} %copy.281), calls=%async_computation.2 | async-start | bytes 2359296 | tf_op jit(solution)/shard_map/all_to_all | solution.py:92
  136.8 62.3 %copy-start.73 = (f32[4,128]{1,0:T(4,128)}, f32[4,128]{1,0:T(4,128)S(1)}, u32[]{:S(2)}) copy-start(f32[4,128]{1,0:T(4,128)S(1)} %broadcast_multiply_fusion.2) | copy-start | bytes 6148
  255.6 21.5 %all-to-all-start = ((bf16[1,1,4,8,16,1152]{5,4,2,1,0,3:T(8,128)(2,1)}), bf16[1,1,4,8,16,1152]{5,4,2,1,0,3:T(8,128)(2,1)S(1)}, u32[]{:S(2)}, u32[]{:S(2)}) async-start(bf16[1,1,4,8,16,1152]{5,4,2,1,0,3:T(8,128)(2,1)} %copy.260), calls=%async_computation | async-start | bytes 2359296 | tf_op jit(solution)/shard_map/all_to_all | solution.py:92
  259.3 138.6 %copy-start.98 = (f32[1152]{0:T(1024)}, f32[1152]{0:T(1024)S(1)}, u32[]{:S(2)}) copy-start(f32[1152]{0:T(1024)S(1)} %get-tuple-element.26) | copy-start | bytes 13828
  259.3 238.2 %copy-start.66 = (f32[1152]{0:T(1024)}, f32[1152]{0:T(1024)S(1)}, u32[]{:S(2)}) copy-start(f32[1152]{0:T(1024)S(1)} %get-tuple-element.27) | copy-start | bytes 13828
  259.3 238.2 %copy-start.68 = (f32[1152]{0:T(1024)}, f32[1152]{0:T(1024)S(1)}, u32[]{:S(2)}) copy-start(f32[1152]{0:T(1024)S(1)} %get-tuple-element.25) | copy-start | bytes 13828
  361.7 135.8 %copy-start.51 = (f32[32,16]{1,0:T(8,128)}, f32[32,16]{1,0:T(8,128)S(1)}, u32[]{:S(2)}) copy-start(f32[32,16]{1,0:T(8,128)S(1)} %copy.275) | copy-start | bytes 6148
  363.9 133.6 %copy-start.61 = (f32[32,16]{1,0:T(8,128)}, f32[32,16]{1,0:T(8,128)S(1)}, u32[]{:S(2)}) copy-start(f32[32,16]{1,0:T(8,128)S(1)} %copy.277) | copy-start | bytes 6148
  586.0 20.3 %all-to-all-start.3 = ((bf16[8,1,4,1,16,1152]{5,4,2,3,1,0:T(8,128)(2,1)}), bf16[8,1,4,1,16,1152]{5,4,2,3,1,0:T(8,128)(2,1)S(1)}, u32[]{:S(2)}, u32[]{:S(2)}) async-start(bf16[8,1,4,1,16,1152]{5,4,2,3,1,0:T(8,128)(2,1)} %bitcast.346), calls=%async_computation.3 | async-start | bytes 2359296 | tf_op jit(solution)/shard_map/all_to_all | solution.py:114
  589.5 234.3 %reduce-scatter.19.cloned.1.call-start = ((), (), s32[]{:S(2)}) async-start(), calls=%async_computation.25 | async-start | bytes 2985984 | tf_op jit(solution)/shard_map/reduce_scatter | solution.py:264
  602.3 221.5 %reduce-scatter.11.cloned.1.call-start = ((), (), s32[]{:S(2)}) async-start(), calls=%async_computation.21 | async-start | bytes 2985984 | tf_op jit(solution)/shard_map/reduce_scatter | solution.py:264
  645.7 178.1 %reduce-scatter.17.cloned.1.call-start = ((), (), s32[]{:S(2)}) async-start(), calls=%async_computation.24 | async-start | bytes 8957952 | tf_op jit(solution)/shard_map/reduce_scatter | solution.py:264
  657.0 187.1 %reduce-scatter.9.cloned.1.call-start = ((), (), s32[]{:S(2)}) async-start(), calls=%async_computation.20 | async-start | bytes 8957952 | tf_op jit(solution)/shard_map/reduce_scatter | solution.py:264
  703.0 5.3 collective-permute-start.1
  730.9 199.0 %reduce-scatter.23.cloned.1.call-start = ((), (), s32[]{:S(2)}) async-start(), calls=%async_computation.27 | async-start | bytes 11943936 | tf_op jit(solution)/shard_map/reduce_scatter | solution.py:264
  745.1 270.3 %reduce-scatter.21.cloned.1.call-start = ((), (), s32[]{:S(2)}) async-start(), calls=%async_computation.26 | async-start | bytes 11943936 | tf_op jit(solution)/shard_map/reduce_scatter | solution.py:264
  757.0 344.0 %reduce-scatter.15.cloned.1.call-start = ((), (), s32[]{:S(2)}) async-start(), calls=%async_computation.23 | async-start | bytes 11943936 | tf_op jit(solution)/shard_map/reduce_scatter | solution.py:264
  770.6 416.0 %reduce-scatter.13.cloned.1.call-start = ((), (), s32[]{:S(2)}) async-start(), calls=%async_computation.22 | async-start | bytes 11943936 | tf_op jit(solution)/shard_map/reduce_scatter | solution.py:264
  782.9 821.1 %all-reduce.5.cloned.1.call-start = ((), (), s32[]{:S(2)}) async-start(), calls=%async_computation.28 | async-start | bytes 23887872 | tf_op jit(solution)/shard_map/psum | solution.py:344
  (99 other events, 746.2 us)
Sparse Core Ops, SparseCore 0:
  9.9 55.5 all-gather.8
  67.4 38.6 all-gather.10
  108.1 66.9 all-gather.12
  176.8 63.8 all-gather.14
  242.4 57.9 all-gather.16
  302.2 29.9 all-gather.18
  334.1 63.8 all-gather.20
  399.8 63.8 all-gather.22
  602.4 45.0 reduce-scatter.18
  651.8 43.7 reduce-scatter.10
  699.2 70.5 reduce-scatter.16
  773.5 70.5 reduce-scatter.8
  847.6 82.1 reduce-scatter.22
  933.2 82.2 reduce-scatter.20
  1018.8 82.2 reduce-scatter.14
  1104.4 82.2 reduce-scatter.12
  1191.6 412.4 all-reduce.4
where the time goes:
time: 1640 us; the launch traced here: 1630 us
  waiting for transfers between devices  963 us (59%)
  matrix products  338 us (21%)
  local copies, waits for them, and re-layouts  141 us (9%)
  other arithmetic  90 us (5%)
  blocking collectives  69.6 us (4%)
    psum x1, waiting for transfers between devices, per_device(): lax.psum(mod_weight_one.astype(jnp.bfloat16), 'rep').astype(jnp.float32)  387 us
    reduce_scatter x8, waiting for transfers between devices, spread_rows_out(): lax.psum_scatter(jnp.einsum('nd,ne->de', left_flat, right_flat, preferred...  363 us
    dot_general x8, matrix products, project(): jnp.einsum('csld,de->csle', left_operand, right_operand, preferred_elemen...  99 us
    all_gather x2, waiting for transfers between devices, gather_layer(): lax.all_gather(down_w, 'seq', axis=0, tiled=True)  94.2 us
    dot_general x8, matrix products, project_back(): jnp.einsum('csle,de->csld', incoming, right_operand, preferred_element_ty...  87.1 us
    dot_general x8, matrix products, spread_rows_out(): jnp.einsum('nd,ne->de', left_flat, right_flat, preferred_element_type=jnp...  76.2 us
    all_gather x2, waiting for transfers between devices, gather_layer(): lax.all_gather(up_w, 'seq', axis=0, tiled=True)  70.6 us
  transfers between devices with their start and end apart: 22, of which 14 were waited for; matrix products, arithmetic and copies ran while one was open for 25% of the time, Pallas kernels for 0%

commit v1 on v0

--- a/solution.py
+++ b/solution.py
@@ -6,6 +6,32 @@
 HEADS = 16
 HEAD_WIDTH = 72
 norm_epsilon = 1e-06
+
+
+def order_turns_up(own_rows):
+    dev_axis = "seq"
+    newest = lax.axis_size(dev_axis)
+    seen_now = lax.axis_index(dev_axis)
+    vec_out, h_now, finding = (newest, seen_now, own_rows.shape[0])
+    q_next = jnp.zeros(
+        [dev_j * vec_out if num == 0 else dev_j for num, dev_j in enumerate(own_rows.shape)],
+        own_rows.dtype,
+    )
+    current_arr = lax.dynamic_update_slice_in_dim(q_next, own_rows, h_now * finding, axis=0)
+    b_next = outcome_arr = own_rows
+    for nth in range(1, vec_out // 2 + 1):
+        mid_arr = list(map(lambda num: (num, (num + 1) % vec_out), range(vec_out)))
+        b_next = lax.ppermute(b_next, dev_axis, mid_arr)
+        current_arr = lax.dynamic_update_slice_in_dim(
+            current_arr, b_next, (h_now - nth) % vec_out * finding, axis=0
+        )
+        if 2 * nth < vec_out:
+            f_now = list(map(lambda num: (num, (num - 1) % vec_out), range(vec_out)))
+            outcome_arr = lax.ppermute(outcome_arr, dev_axis, f_now)
+            current_arr = lax.dynamic_update_slice_in_dim(
+                current_arr, outcome_arr, (h_now + nth) % vec_out * finding, axis=0
+            )
+    return current_arr
 
 
 def from_partner(block, axis, apart):
@@ -64,7 +90,7 @@
         lax.all_gather(qkv_w, "seq", axis=0, tiled=True),
         lax.all_gather(out_w, "seq", axis=0, tiled=True),
         lax.all_gather(up_w, "seq", axis=0, tiled=True),
-        lax.all_gather(down_w, "seq", axis=0, tiled=True),
+        order_turns_up(down_w),
     )
 
 

time: 1640 us -> 1720 us (1.049)
  waiting for transfers between devices: 963 us -> 861 us
  local copies, waits for them, and re-layouts: 141 us -> 207 us
  blocking collectives: 69.6 us -> 112 us
  matrix products: 338 us -> 376 us
  starting transfers between devices: 13.1 us -> 34 us
    ppermute x0 -> x14, waiting for transfers between devices: none -> 202 us  [the longest x8 139 us: order_turns_up(): b_next = lax.ppermute(b_next, dev_axis, mid_arr)]
    reduce_scatter x8, waiting for transfers between devices: 363 us -> 258 us  [spread_rows_out(): lax.psum_scatter(jnp.einsum('nd,ne->de', left_flat, right_flat, preferred...]
    psum x1, waiting for transfers between devices: 387 us -> 289 us  [per_device(): lax.psum(mod_weight_one.astype(jnp.bfloat16), 'rep').astype(jnp.float32)]
    all_gather x2, waiting for transfers between devices: 70.6 us -> 24.4 us  [gather_layer(): lax.all_gather(up_w, 'seq', axis=0, tiled=True)]
    all_gather x2, waiting for transfers between devices: 94.2 us -> 55.7 us  [gather_layer_again(): lax.all_gather(down_w, 'seq', axis=0, tiled=True)]
    psum x1, blocking collectives: 26.8 us -> 64.6 us  [modulations(): summed = lax.psum((part_one, part_two), 'seq')]
    dot_general x8 -> x12, matrix products: 99 us -> 136 us  [project(): jnp.einsum('csld,de->csle', left_operand, right_operand, preferred_elemen...]
    all_gather x2, waiting for transfers between devices: 30.5 us -> 0.01 us  [gather_layer(): lax.all_gather(qkv_w, 'seq', axis=0, tiled=True)]
  transfers between devices with their start and end apart: 22 -> 37, of which waited for: 14 -> 20; matrix products, arithmetic and copies ran while one was open for 25% -> 32% of each run, Pallas kernels for 0% -> 0%
where the time goes in v1:
time: 1720 us; the launch traced here: 1710 us
  waiting for transfers between devices  861 us (50%)
  matrix products  376 us (22%)
  local copies, waits for them, and re-layouts  207 us (12%)
  blocking collectives  112 us (7%)
  other arithmetic  107 us (6%)
  starting transfers between devices  34 us (2%)
    psum x1, waiting for transfers between devices, per_device(): lax.psum(mod_weight_one.astype(jnp.bfloat16), 'rep').astype(jnp.float32)  289 us
    reduce_scatter x8, waiting for transfers between devices, spread_rows_out(): lax.psum_scatter(jnp.einsum('nd,ne->de', left_flat, right_flat, preferred...  258 us
    ppermute x8, waiting for transfers between devices, order_turns_up(): b_next = lax.ppermute(b_next, dev_axis, mid_arr)  139 us
    dot_general x12, matrix products, project(): jnp.einsum('csld,de->csle', left_operand, right_operand, preferred_elemen...  136 us
    dot_general x8, matrix products, project_back(): jnp.einsum('csle,de->csld', incoming, right_operand, preferred_element_ty...  82.6 us
    dot_general x8, matrix products, spread_rows_out(): jnp.einsum('nd,ne->de', left_flat, right_flat, preferred_element_type=jnp...  76.7 us
    psum x1, blocking collectives, modulations(): summed = lax.psum((part_one, part_two), 'seq')  64.6 us
    ppermute x6, waiting for transfers between devices, order_turns_up(): outcome_arr = lax.ppermute(outcome_arr, dev_axis, f_now)  62.8 us
  transfers between devices with their start and end apart: 37, of which 20 were waited for; matrix products, arithmetic and copies ran while one was open for 32% of the time, Pallas kernels for 0%

profile of v1, /device:TPU:0, one launch (start us, length us, event | category | flops | bytes accessed | tf_op | source)
XLA Modules:
  0.0 1712.8 jit_solution(18153917742954372537)
XLA Ops:
  25.3 28.0 %collective-permute-done.1 = bf16[576,1152]{1,0:T(8,128)(2,1)} collective-permute-done((bf16[576,1152]{1,0:T(8,128)(2,1)}, bf16[576,1152]{1,0:T(8,128)(2,1)}, u32[]{:S(2)}, u32[]{:S(2)}) %collective-permute-start.1) | collective-permute-done | bytes 1327136 | tf_op jit(solution)/shard_map/ppermute | solution.py:24
  57.2 64.6 %all-reduce = (f32[1,6912]{1,0:T(1,128)S(1)}, f32[1,6912]{1,0:T(1,128)S(1)}) all-reduce(f32[1,6912]{1,0:T(1,128)S(1)} %fusion.226, f32[1,6912]{1,0:T(1,128)S(1)} %fusion.224), channel_id=1, replica_groups=mesh['rep'=4,'seq'=8] {'seq'}, use_global_device_ids=true, to_apply=%region_0.1 | all-reduce | flops 13824 | bytes 110592 | tf_op jit(solution)/shard_map/psum | solution.py:84
  144.2 22.3 %collective-permute-done.4 = bf16[576,1152]{1,0:T(8,128)(2,1)} collective-permute-done((bf16[576,1152]{1,0:T(8,128)(2,1)}, bf16[576,1152]{1,0:T(8,128)(2,1)}, u32[]{:S(2)}, u32[]{:S(2)}) %collective-permute-start.4) | collective-permute-done | bytes 1327136 | tf_op jit(solution)/shard_map/ppermute | solution.py:30
  182.4 37.5 %collective-permute-done.6 = bf16[576,1152]{1,0:T(8,128)(2,1)S(1)} collective-permute-done((bf16[576,1152]{1,0:T(8,128)(2,1)}, bf16[576,1152]{1,0:T(8,128)(2,1)S(1)}, u32[]{:S(2)}, u32[]{:S(2)}) %collective-permute-start.6) | collective-permute-done | bytes 1327136 | tf_op jit(solution)/shard_map/ppermute | solution.py:30
  251.4 21.9 %fusion.181 = bf16[4,16,72,128]{3,2,1,0:T(8,128)(2,1)} fusion(bf16[1,4,128,16,72]{2,4,3,1,0:T(8,128)(2,1)} %bitcast.429, bf16[1,4,128,16,72]{2,4,3,1,0:T(8,128)(2,1)} %bitcast.427, f32[4,16,128]{2,1,0:T(8,128)S(1)} %get-tuple-element.80, f32[4,16,128,256]{3,2,1,0:T(8,128)} %copy-done.10), kind=kOutput, calls=%fused_computation.225 | convolution fusion | flops 317792512 | bytes 11960320 | tf_op jit(solution)/shard_map/cshlm,csmhe->cslhe/dot_general | solution.py:168
  280.9 12.8 fusion.29
  296.9 13.8 add_convert_fusion.3
  315.4 12.9 fusion.116
  350.5 17.0 all-to-all-done
  409.3 16.3 fusion.265
  442.4 24.3 %all-gather.19.cloned.1.call-done = bf16[1152,4608]{1,0:T(8,128)(2,1)} async-done(((bf16[144,4608]{1,0:T(8,128)(2,1)}), bf16[1152,4608]{1,0:T(8,128)(2,1)}) %all-gather.19.cloned.1.call-update) | async-done | bytes 10616848 | tf_op jit(solution)/shard_map/all_gather | solution.py:92
  466.8 13.2 fusion.21
  479.9 52.6 %all-gather.21.cloned.1.call-done = bf16[4608,1152]{1,0:T(8,128)(2,1)} async-done(((bf16[576,1152]{1,0:T(8,128)(2,1)}), bf16[4608,1152]{1,0:T(8,128)(2,1)}) %all-gather.21.cloned.1.call-update) | async-done | bytes 10616848 | tf_op jit(solution)/shard_map/all_gather | solution.py:102
  532.5 15.9 fusion.44
  548.4 12.2 multiply_reduce_fusion.13
  648.1 17.4 %fusion.37 = bf16[4,128,4608]{2,1,0:T(8,128)(2,1)} fusion(f32[4,128,4608]{2,1,0:T(8,128)} %fusion.29, bf16[4608,1152]{1,0:T(8,128)(2,1)} %all-gather.23.cloned.1.call-done, f32[4,128,1152]{2,1,0:T(8,128)S(1)} %bitcast.410, f32[1152]{0:T(1024)S(1)} %copy-done.86), kind=kOutput, calls=%fused_computation.48 | convolution fusion | flops 5484183552 | bytes 27136512 | tf_op jit(solution)/shard_map/csle,de->csld/dot_general | solution.py:69
  665.5 11.9 multiply_reduce_fusion.11
  705.1 21.8 %convolution_bitcast_fusion.6 = f32[1,4,256,16,72]{2,4,3,1,0:T(8,128)} fusion(bf16[4,128,16,72]{1,3,2,0:T(8,128)(2,1)S(1)} %bitcast.432, f32[4,16,128]{2,1,0:T(8,128)S(1)} %copy-done.68, f32[4,16,128,256]{3,2,1,0:T(8,128)} %copy-done.10), kind=kOutput, calls=%fused_computation.198 | convolution fusion | flops 312484096 | bytes 14319616 | tf_op jit(solution)/shard_map/cshlm,cslhe->csmhe/dot_general | solution.py:245
  785.9 13.3 fusion.4
  812.4 12.6 fusion.6
  829.3 43.5 %collective-permute-done.8 = bf16[576,1152]{1,0:T(8,128)(2,1)S(1)} collective-permute-done((bf16[576,1152]{1,0:T(8,128)(2,1)S(1)}, bf16[576,1152]{1,0:T(8,128)(2,1)S(1)}, u32[]{:S(2)}, u32[]{:S(2)}) %collective-permute-start.8) | collective-permute-done | bytes 1327136 | tf_op jit(solution)/shard_map/ppermute | solution.py:24
  878.8 39.4 %collective-permute-done.10 = bf16[576,1152]{1,0:T(8,128)(2,1)} collective-permute-done((bf16[576,1152]{1,0:T(8,128)(2,1)S(1)}, bf16[576,1152]{1,0:T(8,128)(2,1)}, u32[]{:S(2)}, u32[]{:S(2)}) %collective-permute-start.10) | collective-permute-done | bytes 1327136 | tf_op jit(solution)/shard_map/ppermute | solution.py:24
  927.3 23.7 %collective-permute-done.12 = bf16[576,1152]{1,0:T(8,128)(2,1)} collective-permute-done((bf16[576,1152]{1,0:T(8,128)(2,1)}, bf16[576,1152]{1,0:T(8,128)(2,1)}, u32[]{:S(2)}, u32[]{:S(2)}) %collective-permute-start.12) | collective-permute-done | bytes 1327136 | tf_op jit(solution)/shard_map/ppermute | solution.py:24
  952.9 16.6 fusion.185
  981.7 28.0 %all-reduce.1 = (bf16[6912]{0:T(1024)(128)(2,1)S(1)}, bf16[6912]{0:T(1024)(128)(2,1)S(1)}) all-reduce(bf16[6912]{0:T(1024)(128)(2,1)S(1)} %reduce.91, bf16[6912]{0:T(1024)(128)(2,1)S(1)} %reduce.92), channel_id=1, replica_groups=mesh['rep'=4,'seq'=8] {'seq'}, use_global_device_ids=true, to_apply=%region_36.37 | all-reduce | flops 13824 | bytes 55296 | tf_op jit(solution)/shard_map/psum | solution.py:352
  1013.5 85.6 %reduce-scatter.23.cloned.1.call-done = bf16[576,1152]{1,0:T(8,128)(2,1)} async-done(((bf16[4608,1152]{1,0:T(8,128)(2,1)}), bf16[576,1152]{1,0:T(8,128)(2,1)}) %reduce-scatter.23.cloned.1.call-update) | async-done | bytes 1327120 | tf_op jit(solution)/shard_map/reduce_scatter | solution.py:290
  1099.0 85.6 %reduce-scatter.13.cloned.1.call-done = bf16[144,4608]{1,0:T(8,128)(2,1)} async-done(((bf16[1152,4608]{1,0:T(8,128)(2,1)}), bf16[144,4608]{1,0:T(8,128)(2,1)}) %reduce-scatter.13.cloned.1.call-update) | async-done | bytes 1327120 | tf_op jit(solution)/shard_map/reduce_scatter | solution.py:290
  1184.6 85.6 %reduce-scatter.15.cloned.1.call-done = bf16[576,1152]{1,0:T(8,128)(2,1)} async-done(((bf16[4608,1152]{1,0:T(8,128)(2,1)}), bf16[576,1152]{1,0:T(8,128)(2,1)}) %reduce-scatter.15.cloned.1.call-update) | async-done | bytes 1327120 | tf_op jit(solution)/shard_map/reduce_scatter | solution.py:290
  1314.0 16.3 fusion.263
  1345.0 22.2 %fusion.113 = bf16[32,16,1152]{2,1,0:T(8,128)(2,1)} fusion(f32[32,16,1152]{2,1,0:T(8,128)} %copy-done.40, bf16[4608,1152]{1,0:T(8,128)(2,1)} %constant_dynamic-update-slice_fusion.15, bf16[1152,4608]{1,0:T(8,128)(2,1)} %all-gather.19.cloned.1.call-done, f32[1152]{0:T(1024)S(1)} %copy-done.115, f32[1152]{0:T(1024)S(1)} %copy-done.71, ...), kind=kOutput, calls=%fused_computation.120 | convolution fusion | flops 10897588224 | bytes 24790528 | tf_op jit(solution)/shard_map/csld,de->csle/dot_general | solution.py:63
  1372.0 19.8 %all_to_all.20 = bf16[8,1,4,1,16,1152]{5,4,2,3,1,0:T(8,128)(2,1)S(1)} all-to-all(bf16[8,1,4,1,16,1152]{5,4,2,3,1,0:T(8,128)(2,1)S(1)} %bitcast.421), channel_id=1, replica_groups=mesh['rep'=4,'seq'=8] {'seq'}, dimensions={0} | all-to-all | bytes 2359296 | tf_op jit(solution)/shard_map/all_to_all | solution.py:140
  1398.3 289.3 %all-reduce.5.cloned.1.call-done = (bf16[144,6912]{1,0:T(8,128)(2,1)}, bf16[144,3456]{1,0:T(8,128)(2,1)}, bf16[144,1152]{1,0:T(8,128)(2,1)}, bf16[144,4608]{1,0:...) async-done(((bf16[144,6912]{1,0:T(8,128)(2,1)}, ...) | async-done | bytes 11943952 | tf_op jit(solution)/shard_map/psum | solution.py:370
  (543 shorter events, 499.0 us)
Async XLA Ops:
  7.2 116.4 %all-gather.9.cloned.1.call-start = ((), (), s32[]{:S(2)}) async-start(), calls=%async_computation.13 | async-start | bytes 8957952 | tf_op jit(solution)/shard_map/all_gather | solution.py:90
  7.9 265.4 %all-gather.11.cloned.1.call-start = ((), (), s32[]{:S(2)}) async-start(), calls=%async_computation.14 | async-start | bytes 2985984 | tf_op jit(solution)/shard_map/all_gather | solution.py:91
  8.7 272.2 %all-gather.13.cloned.1.call-start = ((), (), s32[]{:S(2)}) async-start(), calls=%async_computation.15 | async-start | bytes 11943936 | tf_op jit(solution)/shard_map/all_gather | solution.py:92
  9.4 287.5 %all-gather.23.cloned.1.call-start = ((), (), s32[]{:S(2)}) async-start(), calls=%async_computation.20 | async-start | bytes 11943936 | tf_op jit(solution)/shard_map/all_gather | solution.py:102
  10.0 368.8 %all-gather.15.cloned.1.call-start = ((), (), s32[]{:S(2)}) async-start(), calls=%async_computation.16 | async-start | bytes 8957952 | tf_op jit(solution)/shard_map/all_gather | solution.py:90
  10.6 422.8 %all-gather.17.cloned.1.call-start = ((), (), s32[]{:S(2)}) async-start(), calls=%async_computation.17 | async-start | bytes 2985984 | tf_op jit(solution)/shard_map/all_gather | solution.py:91
  11.2 455.6 %all-gather.19.cloned.1.call-start = ((), (), s32[]{:S(2)}) async-start(), calls=%async_computation.18 | async-start | bytes 11943936 | tf_op jit(solution)/shard_map/all_gather | solution.py:92
  11.9 41.4 %collective-permute-start.1 = (bf16[576,1152]{1,0:T(8,128)(2,1)}, bf16[576,1152]{1,0:T(8,128)(2,1)}, u32[]{:S(2)}, u32[]{:S(2)}) collective-permute-start(bf16[576,1152]{1,0:T(8,128)(2,1)} %param.19), channel_id=1, source_target_pairs={{0,1},{1,2},{2,3},{3,4},{4,5},{5,6},{6,7},{7,0},{8,9},{9,10},{10,1... | collective-permute-start | bytes 3981320 | tf_op jit(solution)/shard_map/ppermute | solution.py:24
  12.4 110.2 %collective-permute-start.2 = (bf16[576,1152]{1,0:T(8,128)(2,1)}, bf16[576,1152]{1,0:T(8,128)(2,1)}, u32[]{:S(2)}, u32[]{:S(2)}) collective-permute-start(bf16[576,1152]{1,0:T(8,128)(2,1)} %param.19), channel_id=1, source_target_pairs={{0,7},{1,0},{2,1},{3,2},{4,3},{5,4},{6,5},{7,6},{8,15},{9,8},{10,9... | collective-permute-start | bytes 3981320 | tf_op jit(solution)/shard_map/ppermute | solution.py:30
  18.3 293.6 %all-to-all-start.2 = ((bf16[1,1,4,8,16,1152]{5,4,2,1,0,3:T(8,128)(2,1)}), bf16[1,1,4,8,16,1152]{5,4,2,1,0,3:T(8,128)(2,1)}, u32[]{:S(2)}, u32[]{:S(2)}) async-start(bf16[1,1,4,8,16,1152]{5,4,2,1,0,3:T(8,128)(2,1)} %copy.326), calls=%async_computation.2 | async-start | bytes 2359296 | tf_op jit(solution)/shard_map/all_to_all | solution.py:118
  22.6 509.9 %all-gather.21.cloned.1.call-start = ((), (), s32[]{:S(2)}) async-start(), calls=%async_computation.19 | async-start | bytes 11943936 | tf_op jit(solution)/shard_map/all_gather | solution.py:102
  53.3 70.3 %collective-permute-start.3 = (bf16[576,1152]{1,0:T(8,128)(2,1)}, bf16[576,1152]{1,0:T(8,128)(2,1)}, u32[]{:S(2)}, u32[]{:S(2)}) collective-permute-start(bf16[576,1152]{1,0:T(8,128)(2,1)} %collective-permute-done.1), channel_id=1, source_target_pairs={{0,1},{1,2},{2,3},{3,4},{4,5},{5,6},{6,7},{7,0},{8,9},{9,10},{10,1... | collective-permute-start | bytes 3981320 | tf_op jit(solution)/shard_map/ppermute | solution.py:24
  122.7 43.8 %collective-permute-start.4 = (bf16[576,1152]{1,0:T(8,128)(2,1)}, bf16[576,1152]{1,0:T(8,128)(2,1)}, u32[]{:S(2)}, u32[]{:S(2)}) collective-permute-start(bf16[576,1152]{1,0:T(8,128)(2,1)} %collective-permute-done.2), channel_id=1, source_target_pairs={{0,7},{1,0},{2,1},{3,2},{4,3},{5,4},{6,5},{7,6},{8,15},{9,8},{10,9... | collective-permute-start | bytes 3981320 | tf_op jit(solution)/shard_map/ppermute | solution.py:30
  123.6 48.2 %collective-permute-start.5 = (bf16[576,1152]{1,0:T(8,128)(2,1)}, bf16[576,1152]{1,0:T(8,128)(2,1)}, u32[]{:S(2)}, u32[]{:S(2)}) collective-permute-start(bf16[576,1152]{1,0:T(8,128)(2,1)} %collective-permute-done.3), channel_id=1, source_target_pairs={{0,1},{1,2},{2,3},{3,4},{4,5},{5,6},{6,7},{7,0},{8,9},{9,10},{10,1... | collective-permute-start | bytes 3981320 | tf_op jit(solution)/shard_map/ppermute | solution.py:24
  136.2 97.8 %collective-permute-start = (bf16[2,1,4,128,1152]{4,3,2,1,0:T(8,128)(2,1)}, bf16[2,1,4,128,1152]{4,3,2,1,0:T(8,128)(2,1)}, u32[]{:S(2)}, u32[]{:S(2)}) collective-permute-start(bf16[2,1,4,128,1152]{4,3,2,1,0:T(8,128)(2,1)} %pad_maximum_fusion.1), channel_id=1, source_target_pairs={{0,1},{1,0},{2,3},{3,2},{4,5},{5,4},{6,7},{7,6},{8,9},{9,8},{10,11... | collective-permute-start | bytes 7077896 | tf_op jit(solution)/shard_map/ppermute | solution.py:44
  166.5 53.4 %collective-permute-start.6 = (bf16[576,1152]{1,0:T(8,128)(2,1)}, bf16[576,1152]{1,0:T(8,128)(2,1)S(1)}, u32[]{:S(2)}, u32[]{:S(2)}) collective-permute-start(bf16[576,1152]{1,0:T(8,128)(2,1)} %collective-permute-done.4), channel_id=1, source_target_pairs={{0,7},{1,0},{2,1},{3,2},{4,3},{5,4},{6,5},{7,6},{8,15},{9,8},{10,9... | collective-permute-start | bytes 3981320 | tf_op jit(solution)/shard_map/ppermute | solution.py:30
  171.8 53.9 %collective-permute-start.7 = (bf16[576,1152]{1,0:T(8,128)(2,1)}, bf16[576,1152]{1,0:T(8,128)(2,1)S(1)}, u32[]{:S(2)}, u32[]{:S(2)}) collective-permute-start(bf16[576,1152]{1,0:T(8,128)(2,1)} %collective-permute-done.5), channel_id=1, source_target_pairs={{0,1},{1,2},{2,3},{3,4},{4,5},{5,6},{6,7},{7,0},{8,9},{9,10},{10,1... | collective-permute-start | bytes 3981320 | tf_op jit(solution)/shard_map/ppermute | solution.py:24
  333.3 34.2 %all-to-all-start = ((bf16[1,1,4,8,16,1152]{5,4,2,1,0,3:T(8,128)(2,1)}), bf16[1,1,4,8,16,1152]{5,4,2,1,0,3:T(8,128)(2,1)}, u32[]{:S(2)}, u32[]{:S(2)}) async-start(bf16[1,1,4,8,16,1152]{5,4,2,1,0,3:T(8,128)(2,1)} %copy.309), calls=%async_computation | async-start | bytes 2359296 | tf_op jit(solution)/shard_map/all_to_all | solution.py:118
  631.2 381.0 %reduce-scatter.19.cloned.1.call-start = ((), (), s32[]{:S(2)}) async-start(), calls=%async_computation.26 | async-start | bytes 2985984 | tf_op jit(solution)/shard_map/reduce_scatter | solution.py:290
  643.9 368.3 %reduce-scatter.11.cloned.1.call-start = ((), (), s32[]{:S(2)}) async-start(), calls=%async_computation.22 | async-start | bytes 2985984 | tf_op jit(solution)/shard_map/reduce_scatter | solution.py:290
  687.2 325.0 %reduce-scatter.17.cloned.1.call-start = ((), (), s32[]{:S(2)}) async-start(), calls=%async_computation.25 | async-start | bytes 8957952 | tf_op jit(solution)/shard_map/reduce_scatter | solution.py:290
  698.5 313.7 %reduce-scatter.9.cloned.1.call-start = ((), (), s32[]{:S(2)}) async-start(), calls=%async_computation.21 | async-start | bytes 8957952 | tf_op jit(solution)/shard_map/reduce_scatter | solution.py:290
  771.1 242.4 %reduce-scatter.21.cloned.1.call-start = ((), (), s32[]{:S(2)}) async-start(), calls=%async_computation.27 | async-start | bytes 11943936 | tf_op jit(solution)/shard_map/reduce_scatter | solution.py:290
  783.2 315.8 %reduce-scatter.23.cloned.1.call-start = ((), (), s32[]{:S(2)}) async-start(), calls=%async_computation.28 | async-start | bytes 11943936 | tf_op jit(solution)/shard_map/reduce_scatter | solution.py:290
  799.2 385.4 %reduce-scatter.13.cloned.1.call-start = ((), (), s32[]{:S(2)}) async-start(), calls=%async_computation.23 | async-start | bytes 11943936 | tf_op jit(solution)/shard_map/reduce_scatter | solution.py:290
  810.9 459.3 %reduce-scatter.15.cloned.1.call-start = ((), (), s32[]{:S(2)}) async-start(), calls=%async_computation.24 | async-start | bytes 11943936 | tf_op jit(solution)/shard_map/reduce_scatter | solution.py:290
  825.0 862.6 %all-reduce.5.cloned.1.call-start = ((), (), s32[]{:S(2)}) async-start(), calls=%async_computation.29 | async-start | bytes 23887872 | tf_op jit(solution)/shard_map/psum | solution.py:370
  826.6 46.2 %collective-permute-start.8 = (bf16[576,1152]{1,0:T(8,128)(2,1)S(1)}, bf16[576,1152]{1,0:T(8,128)(2,1)S(1)}, u32[]{:S(2)}, u32[]{:S(2)}) collective-permute-start(bf16[576,1152]{1,0:T(8,128)(2,1)S(1)} %copy-done.36), channel_id=1, source_target_pairs={{0,1},{1,2},{2,3},{3,4},{4,5},{5,6},{6,7},{7,0},{8,9},{9,10},{10,1... | collective-permute-start | bytes 3981320 | tf_op jit(solution)/shard_map/ppermute | solution.py:24
  826.6 49.3 %collective-permute-start.9 = (bf16[576,1152]{1,0:T(8,128)(2,1)S(1)}, bf16[576,1152]{1,0:T(8,128)(2,1)}, u32[]{:S(2)}, u32[]{:S(2)}) collective-permute-start(bf16[576,1152]{1,0:T(8,128)(2,1)S(1)} %copy-done.36), channel_id=1, source_target_pairs={{0,7},{1,0},{2,1},{3,2},{4,3},{5,4},{6,5},{7,6},{8,15},{9,8},{10,9... | collective-permute-start | bytes 3981320 | tf_op jit(solution)/shard_map/ppermute | solution.py:30
  872.8 45.5 %collective-permute-start.10 = (bf16[576,1152]{1,0:T(8,128)(2,1)S(1)}, bf16[576,1152]{1,0:T(8,128)(2,1)}, u32[]{:S(2)}, u32[]{:S(2)}) collective-permute-start(bf16[576,1152]{1,0:T(8,128)(2,1)S(1)} %collective-permute-done.8), channel_id=1, source_target_pairs={{0,1},{1,2},{2,3},{3,4},{4,5},{5,6},{6,7},{7,0},{8,9},{9,10},{10,1... | collective-permute-start | bytes 3981320 | tf_op jit(solution)/shard_map/ppermute | solution.py:24
  875.9 43.5 %collective-permute-start.11 = (bf16[576,1152]{1,0:T(8,128)(2,1)}, bf16[576,1152]{1,0:T(8,128)(2,1)}, u32[]{:S(2)}, u32[]{:S(2)}) collective-permute-start(bf16[576,1152]{1,0:T(8,128)(2,1)} %collective-permute-done.9), channel_id=1, source_target_pairs={{0,7},{1,0},{2,1},{3,2},{4,3},{5,4},{6,5},{7,6},{8,15},{9,8},{10,9... | collective-permute-start | bytes 3981320 | tf_op jit(solution)/shard_map/ppermute | solution.py:30
  951.0 319.3 %collective-permute-start.14 = (bf16[576,1152]{1,0:T(8,128)(2,1)}, bf16[576,1152]{1,0:T(8,128)(2,1)}, u32[]{:S(2)}, u32[]{:S(2)}) collective-permute-start(bf16[576,1152]{1,0:T(8,128)(2,1)} %collective-permute-done.12), channel_id=1, source_target_pairs={{0,1},{1,2},{2,3},{3,4},{4,5},{5,6},{6,7},{7,0},{8,9},{9,10},{10,1... | collective-permute-start | bytes 3981320 | tf_op jit(solution)/shard_map/ppermute | solution.py:24
  (133 other events, 4343.7 us)
Sparse Core Ops, SparseCore 0:
  9.9 86.2 all-gather.8
  98.1 32.8 all-gather.10
  132.9 95.9 all-gather.12
  230.6 66.2 all-gather.22
  298.6 70.5 all-gather.14
  371.0 30.0 all-gather.16
  402.9 63.8 all-gather.18
  468.6 63.8 all-gather.20
  644.0 45.1 reduce-scatter.18
  693.5 43.7 reduce-scatter.10
  740.8 70.0 reduce-scatter.16
  814.7 100.5 reduce-scatter.8
  918.8 94.6 reduce-scatter.20
  1016.8 82.1 reduce-scatter.22
  1102.4 82.1 reduce-scatter.12
  1188.0 82.2 reduce-scatter.14
  1275.1 412.4 all-reduce.4
